TPU v7x, 32 devices: a whole 2x2x4 slice. The times are simulated.
32 devices in a mesh: seq: 8 (over z, x), head: 4 (over y, core).
Axes of the slice: x: 2, y: 2, z: 4, core: 2. Of those that a mesh axis runs over, the one named last changes fastest.
Arguments:
- queries: bfloat16 [8192, 2048], P('seq', 'head'), may hold values from -6 to 6
- key_vectors: bfloat16 [8192, 2048], P('seq', 'head'), may hold values from -0.52734375 to 0.52734375
- value_vectors: bfloat16 [8192, 2048], P('seq', 'head'), may hold values from -6 to 6
- out_grad: bfloat16 [8192, 2048], P('seq', 'head'), may hold values from -6 to 6
- head_rates: float32 [16], P('head'), may hold values from 6.1035156e-05 to 0.05
- gate_scale: float32 [16, 8192], P('head', 'seq'), may hold values from 0.5 to 2
Outputs:
- query_gradient: bfloat16 [8192, 2048], P('seq', 'head')
- key_gradient: bfloat16 [8192, 2048], P('seq', 'head')
- value_gradient: bfloat16 [8192, 2048], P('seq', 'head')
All inputs are finite; a program needn't handle non-finite values.
Results may differ from a plain program's by a relative error of at most 0.014.
Values may be sent and summed in bfloat16 or wider, within the bound.
A program may use at most 128 MiB of HBM per device.

v0:
```python
import jax
import jax.numpy as jnp
from jax import lax
from jax.sharding import PartitionSpec as P

EPS = 1e-06


def causal_factor(cumulative):
    length_here = cumulative.shape[1]
    differences = cumulative[:, :, None] - cumulative[:, None, :]
    lower_mask = jnp.tril(jnp.ones((length_here, length_here), dtype=bool))[None]
    return jnp.where(lower_mask, jnp.exp(jnp.where(lower_mask, differences, 0.0)), 0.0)


def block_weights(totals):
    running = jnp.cumsum(totals, axis=0)
    ahead = running - totals
    index = jnp.arange(totals.shape[0])
    mask = (index[None, :] > index[:, None])[:, :, None]
    exponent = ahead[None, :, :] - running[:, None, :]
    return jnp.where(mask, jnp.exp(jnp.where(mask, exponent, 0.0)), 0.0)


def body(queries, key_vectors, value_vectors, out_grad, head_rates, gate_scale):
    heads = gate_scale.shape[0]
    tokens_here = gate_scale.shape[1]
    depth_key = queries.shape[1] // heads
    depth_value = value_vectors.shape[1] // heads
    count = lax.axis_size("seq")
    query_block = queries.reshape(tokens_here, heads, depth_key)
    key_tile_block = key_vectors.reshape(tokens_here, heads, depth_key)
    value_tile_block = value_vectors.reshape(tokens_here, heads, depth_value)
    grad_block = out_grad.reshape(tokens_here, heads, depth_value)
    cumulative = jnp.cumsum(-head_rates[:, None] * gate_scale, axis=1)
    overall = cumulative[:, -1]
    trailing_portion = jnp.exp(overall[:, None] - cumulative).T[:, :, None]
    head_exponential = jnp.exp(cumulative).T[:, :, None]
    damped_key_rows = (key_tile_block.astype(jnp.float32) * trailing_portion).astype(jnp.bfloat16)
    state_increment = jnp.einsum(
        "zun,zui->uni", damped_key_rows, value_tile_block, preferred_element_type=jnp.float32
    )
    tiled = jnp.broadcast_to(overall[:, None], (heads, count))
    totals, fragment_list = (
        lax.all_gather(overall[None, :].astype(jnp.bfloat16), "seq", axis=0, tiled=True).astype(
            jnp.float32
        ),
        lax.all_gather(
            state_increment[None].astype(jnp.bfloat16), "seq", axis=0, tiled=True
        ).astype(jnp.float32),
    )
    position = lax.axis_index("seq")
    running = jnp.cumsum(totals, axis=0)
    before = lax.dynamic_index_in_dim(running, position, 0, keepdims=False) - overall
    earlier_mask = (jnp.arange(totals.shape[0]) < position)[:, None]
    exponent = jnp.where(earlier_mask, before[None, :] - running, 0.0)
    carried_weight_matrix = jnp.where(earlier_mask, jnp.exp(exponent), 0.0)
    leading_portion = jnp.einsum(
        "pg,pgoq->goq", carried_weight_matrix, fragment_list, precision=lax.Precision.HIGHEST
    )
    damped_query_rows = (query_block.astype(jnp.float32) * head_exponential).astype(jnp.bfloat16)
    factor = causal_factor(cumulative)
    scores = jnp.einsum(
        "thk,shk->hts", query_block, key_tile_block, preferred_element_type=jnp.float32
    )
    attn_weights = (scores * factor).astype(jnp.bfloat16)
    state_portion = leading_portion.astype(jnp.bfloat16)
    output_result = jnp.einsum(
        "gqw,qwx->gqx", damped_query_rows, state_portion, preferred_element_type=jnp.float32
    )
    output_result = output_result + jnp.einsum(
        "hts,shv->thv", attn_weights, value_tile_block, preferred_element_type=jnp.float32
    )
    grad_full = grad_block.astype(jnp.float32)
    square_sum, cross_sum = lax.psum(
        (
            jnp.sum(output_result * output_result, axis=(1, 2)),
            jnp.sum(grad_full * output_result, axis=(1, 2)),
        ),
        "head",
    )
    width = heads * lax.axis_size("head") * depth_value
    root = jnp.sqrt(square_sum / width + EPS)
    output_delta = (
        grad_full / root[:, None, None]
        - output_result * (cross_sum / (width * root**3))[:, None, None]
    )
    output_delta = output_delta.astype(jnp.bfloat16)
    gradient_total_sum = jnp.einsum(
        "zun,zui->uni", damped_query_rows, output_delta, preferred_element_type=jnp.float32
    )
    shares, totals = (
        lax.all_to_all(
            gradient_total_sum.reshape(heads, -1).astype(jnp.bfloat16),
            "seq",
            split_axis=1,
            concat_axis=0,
            tiled=True,
        ).astype(jnp.float32),
        lax.all_to_all(
            tiled.astype(jnp.bfloat16), "seq", split_axis=1, concat_axis=0, tiled=True
        ).astype(tiled.dtype),
    )
    shares = shares.reshape(count, heads, -1)
    weights = block_weights(totals.reshape(count, heads))
    combined = jnp.einsum("cjh,jhw->chw", weights, shares, precision=lax.Precision.HIGHEST)
    returned = lax.all_to_all(
        combined.reshape(count * heads, -1).astype(jnp.bfloat16),
        "seq",
        split_axis=0,
        concat_axis=1,
        tiled=True,
    )
    later = returned.reshape(gradient_total_sum.shape)
    mixed = (
        jnp.einsum(
            "thv,shv->hts", output_delta, value_tile_block, preferred_element_type=jnp.float32
        )
        * factor
    )
    mixed_half = mixed.astype(jnp.bfloat16)
    query_gradient = head_exponential * jnp.einsum(
        "syi,ybi->syb", output_delta, state_portion, preferred_element_type=jnp.float32
    )
    query_gradient = query_gradient + jnp.einsum(
        "hts,shk->thk", mixed_half, key_tile_block, preferred_element_type=jnp.float32
    )
    key_gradient = trailing_portion * jnp.einsum(
        "zxl,xfl->zxf", value_tile_block, later, preferred_element_type=jnp.float32
    )
    key_gradient = key_gradient + jnp.einsum(
        "hts,thk->shk", mixed_half, query_block, preferred_element_type=jnp.float32
    )
    value_gradient = trailing_portion * jnp.einsum(
        "jip,ipa->jia", key_tile_block, later, preferred_element_type=jnp.float32
    )
    value_gradient = value_gradient + jnp.einsum(
        "hts,thv->shv", attn_weights, output_delta, preferred_element_type=jnp.float32
    )
    return (
        query_gradient.astype(jnp.bfloat16).reshape(tokens_here, heads * depth_key),
        key_gradient.astype(jnp.bfloat16).reshape(tokens_here, heads * depth_key),
        value_gradient.astype(jnp.bfloat16).reshape(tokens_here, heads * depth_value),
    )


def solution(mesh):
    placed = (
        P("seq", "head"),
        P("seq", "head"),
        P("seq", "head"),
        P("seq", "head"),
        P("head"),
        P("head", "seq"),
    )
    return jax.shard_map(
        body,
        mesh=mesh,
        in_specs=placed,
        out_specs=(P("seq", "head"), P("seq", "head"), P("seq", "head")),
        check_vma=False,
    )
```

profile of v0, /device:TPU:0, one launch (start us, length us, event | category | flops | bytes accessed | tf_op | source)
XLA Modules:
  0.0 132.0 jit_solution(106515346755941865)
XLA Ops:
  10.6 1.5 %copy.83 = bf16[1024,512]{0,1:T(8,128)(2,1)S(1)} copy(bf16[1024,512]{1,0:T(8,128)(2,1)} %param.7) | data formatting | bytes 2097152 | tf_op args[1]
  13.8 7.3 %all-to-all-start.1 = ((bf16[4,8,1]{0,2,1:T(2,128)(2,1)}), bf16[4,8,1]{0,2,1:T(2,128)(2,1)S(1)}, u32[]{:S(2)}, u32[]{:S(2)}) async-start(bf16[4,8,1]{0,2,1:T(2,128)(2,1)} %broadcast_in_dim.81), calls=%async_computation.1 | async-start | bytes 8192 | tf_op jit(solution)/shard_map/all_to_all | solution.py:100
  21.1 21.0 %all-gather.1 = bf16[8,1,4]{2,1,0:T(2,128)(2,1)S(1)} all-gather(bf16[1,1,4]{2,1,0:T(2,128)(2,1)S(1)} %get-tuple-element.24), channel_id=1, replica_groups=mesh['seq'=8,'head'=4] {'seq'}, dimensions={0}, use_global_device_ids=true | all-gather | bytes 72 | tf_op jit(solution)/shard_map/all_gather | solution.py:45
  42.5 1.5 %copy.86 = bf16[1024,512]{0,1:T(8,128)(2,1)S(1)} copy(bf16[1024,512]{1,0:T(8,128)(2,1)} %param.6) | data formatting | bytes 2097152 | tf_op args[0]
  45.3 7.4 %multiply_convert_fusion.1 = bf16[4,1024,1024]{2,1,0:T(8,128)(2,1)} fusion(bf16[1024,4,128]{0,2,1:T(8,128)(2,1)S(1)} %bitcast.130, bf16[1024,4,128]{0,2,1:T(8,128)(2,1)S(1)} %bitcast.127, f32[4,1024]{1,0:T(4,128)S(1)} %bitcast.143, pred[1024,1024]{1,0:T(8,128)(4,1)S(1)} %iota_compare_fusion), kind=kOutput, calls=%fused_computation.1 | convolution fusion | flops 1094713344 | bytes 11550720 | tf_op jit(solution)/shard_map/thk,shk->hts/dot_general | solution.py:63
  52.7 1.5 %copy.85 = f32[1024,512]{0,1:T(8,128)S(1)} copy(bf16[1024,512]{1,0:T(8,128)(2,1)} %param.9) | data formatting | bytes 3145728 | tf_op jit(solution)/shard_map/convert_element_type | solution.py:74
  54.4 1.9 %all-gather.4.cloned.1.call-done = bf16[32,128,128]{2,1,0:T(8,128)(2,1)} async-done(((bf16[4,128,128]{2,1,0:T(8,128)(2,1)}), bf16[32,128,128]{2,1,0:T(8,128)(2,1)}) %all-gather.4.cloned.1.call-update) | async-done | bytes 1048592 | tf_op jit(solution)/shard_map/all_gather | solution.py:48
  56.3 2.5 %fusion.9 = f32[4,1,128,128]{3,1,2,0:T(1,128)S(1)} fusion(f32[8,4,1,1]{0,2,3,1:T(1,128)S(1)} %copy.107, bf16[8,4,128,128]{3,2,1,0:T(8,128)(2,1)} %bitcast.139), kind=kOutput, calls=%fused_computation.28 | convolution fusion | flops 6291456 | bytes 1310848 | tf_op jit(solution)/shard_map/pg,pgoq->goq/dot_general | solution.py:58
  58.8 1.7 %fusion.12 = f32[4,128,1024]{2,1,0:T(8,128)S(1)} fusion(bf16[1024,4,128]{0,2,1:T(8,128)(2,1)} %bitcast.131, f32[1024,4]{0,1:T(4,128)S(1)} %get-tuple-element.20, f32[4,128,128]{2,1,0:T(8,128)S(1)} %bitcast.137), kind=kOutput, calls=%fused_computation.31 | convolution fusion | flops 135856128 | bytes 3424256 | tf_op jit(solution)/shard_map/gqw,qwx->gqx/dot_general | solution.py:68
  60.5 7.8 %multiply_reduce_fusion.1 = (f32[1024]{0:T(1024)S(1)}, f32[1024]{0:T(1024)S(1)}, f32[1024,4,128]{0,2,1:T(8,128)}) fusion(f32[1024,512]{0,1:T(8,128)S(1)} %copy.85, bf16[4,1024,1024]{2,1,0:T(8,128)(2,1)} %multiply_convert_fusion.1, f32[4,128,1024]{2,1,0:T(8,128)S(1)} %fusion.12, bf16[1024,512]{1,0:T(8,128)(2,1)S(1)} %copy-done), kind=kOutput, calls=%fused_computation.18 | convolution fusion | flops 1076361216 | bytes 15736832 | tf_op jit(solution)/shard_map/hts,shv->thv/dot_general | solution.py:71
  68.3 5.9 %all-reduce = (f32[1024]{0:T(1024)S(1)}, f32[1024]{0:T(1024)S(1)}) all-reduce(f32[1024]{0:T(1024)S(1)} %get-tuple-element.16, f32[1024]{0:T(1024)S(1)} %get-tuple-element.15), channel_id=1, replica_groups=mesh['seq'=8,'head'=4] {'head'}, use_global_device_ids=true, to_apply=%region_6.7 | all-reduce | flops 2048 | bytes 16384 | tf_op jit(solution)/shard_map/psum | solution.py:75
  74.2 2.2 %subtract_convert_fusion = bf16[1024,4,128]{0,2,1:T(8,128)(2,1)S(1)} fusion(f32[1024,4,128]{0,2,1:T(8,128)} %get-tuple-element.25, f32[1024,4,128]{0,2,1:T(8,128)S(1)} %bitcast.125, f32[1024]{0:T(1024)S(1)} %get-tuple-element.22, f32[1024]{0:T(1024)S(1)} %get-tuple-element.21), kind=kLoop, calls=%fused_computation.16 | loop fusion | flops 2097152 | bytes 5251072 | tf_op jit(solution)/shard_map/convert_element_type | solution.py:88
  78.1 7.9 %multiply_convert_fusion = bf16[4,1024,1024]{2,1,0:T(8,128)(2,1)} fusion(bf16[1024,4,128]{0,2,1:T(8,128)(2,1)S(1)} %subtract_convert_fusion, f32[4,1024]{1,0:T(4,128)S(1)} %bitcast.144, pred[1024,1024]{1,0:T(8,128)(4,1)S(1)} %copy-done.9, bf16[1024,512]{1,0:T(8,128)(2,1)S(1)} %copy-done), kind=kOutput, calls=%fused_computation | convolution fusion | flops 1094713344 | bytes 11550720 | tf_op jit(solution)/shard_map/thv,shv->hts/dot_general | solution.py:116
  86.8 3.4 %all-to-all-start = ((bf16[4,8,2048]{2,0,1:T(4,128)(2,1)}), bf16[4,8,2048]{2,0,1:T(4,128)(2,1)S(1)}, u32[]{:S(2)}, u32[]{:S(2)}) async-start(bf16[4,8,2048]{2,0,1:T(4,128)(2,1)} %copy.96), calls=%async_computation | async-start | bytes 262144 | tf_op jit(solution)/shard_map/all_to_all | solution.py:93
  90.2 3.1 %fusion.19 = f32[4,128,1024]{2,1,0:T(8,128)} fusion(bf16[1024,4,128]{0,2,1:T(8,128)(2,1)} %copy-done.3, f32[4,128,128]{2,1,0:T(8,128)S(1)} %bitcast.138), kind=kOutput, calls=%fused_computation.38 | convolution fusion | flops 134283264 | bytes 3407872 | tf_op jit(solution)/shard_map/syi,ybi->syb/dot_general | solution.py:122
  93.2 4.2 %all-to-all-done = bf16[4,8,2048]{2,0,1:T(4,128)(2,1)S(1)} async-done(((bf16[4,8,2048]{2,0,1:T(4,128)(2,1)}), bf16[4,8,2048]{2,0,1:T(4,128)(2,1)S(1)}, u32[]{:S(2)}, u32[]{:S(2)}) %all-to-all-start) | async-done | bytes 131104 | tf_op jit(solution)/shard_map/all_to_all | solution.py:93
  98.5 3.4 %all-to-all-start.2 = ((bf16[8,4,2048]{2,1,0:T(4,128)(2,1)}), bf16[8,4,2048]{2,1,0:T(4,128)(2,1)S(1)}, u32[]{:S(2)}, u32[]{:S(2)}) async-start(bf16[8,4,2048]{2,1,0:T(4,128)(2,1)} %copy.99), calls=%async_computation.2 | async-start | bytes 262144 | tf_op jit(solution)/shard_map/all_to_all | solution.py:107
  101.9 6.9 %fusion.3 = bf16[1024,4,128]{0,2,1:T(8,128)(2,1)S(1)} fusion(f32[4,128,1024]{2,1,0:T(8,128)} %fusion.19, bf16[4,1024,1024]{2,1,0:T(8,128)(2,1)} %multiply_convert_fusion, bf16[1024,4,128]{0,2,1:T(8,128)(2,1)S(1)} %bitcast.128, f32[1024,4]{0,1:T(4,128)S(1)} %get-tuple-element.20), kind=kOutput, calls=%fused_computation.13 | convolution fusion | flops 1075314688 | bytes 12599296 | tf_op jit(solution)/shard_map/hts,shk->thk/dot_general | solution.py:125
  108.8 1.3 %copy.104 = bf16[1024,512]{1,0:T(8,128)(2,1)} copy(bf16[1024,512]{0,1:T(8,128)(2,1)S(1)} %bitcast.136) | data formatting | bytes 2097152
  110.8 1.8 %fusion.5 = f32[4,128,1024]{2,1,0:T(8,128)} fusion(bf16[4,128,128]{2,1,0:T(8,128)(2,1)S(1)} %reshape.148, bf16[1024,512]{1,0:T(8,128)(2,1)S(1)} %copy-done), kind=kOutput, calls=%fused_computation.24 | convolution fusion | flops 134217728 | bytes 3276800 | tf_op jit(solution)/shard_map/zxl,xfl->zxf/dot_general | solution.py:128
  112.6 4.7 %fusion.1 = bf16[1024,4,128]{0,2,1:T(8,128)(2,1)S(1)} fusion(f32[4,128,1024]{2,1,0:T(8,128)S(1)} %fusion.35, bf16[1024,4,128]{0,2,1:T(8,128)(2,1)S(1)} %copy-done.4, bf16[4,1024,1024]{2,1,0:T(8,128)(2,1)} %multiply_convert_fusion.1, f32[1024,4]{0,1:T(4,128)S(1)} %get-tuple-element.19), kind=kOutput, calls=%fused_computation.7 | convolution fusion | flops 1075314688 | bytes 12599296 | tf_op jit(solution)/shard_map/hts,thv->shv/dot_general | solution.py:137
  117.2 1.3 %copy.106 = bf16[1024,512]{1,0:T(8,128)(2,1)} copy(bf16[1024,512]{0,1:T(8,128)(2,1)S(1)} %bitcast.135) | data formatting | bytes 2097152
  118.6 5.3 %fusion.2 = bf16[1024,4,128]{0,2,1:T(8,128)(2,1)S(1)} fusion(f32[4,128,1024]{2,1,0:T(8,128)} %fusion.5, bf16[1024,4,128]{0,2,1:T(8,128)(2,1)S(1)} %bitcast.133, bf16[4,1024,1024]{2,1,0:T(8,128)(2,1)} %multiply_convert_fusion, f32[1024,4]{0,1:T(4,128)S(1)} %get-tuple-element.19), kind=kOutput, calls=%fused_computation.10 | convolution fusion | flops 1075314688 | bytes 12599296 | tf_op jit(solution)/shard_map/hts,thk->shk/dot_general | solution.py:131
  123.8 1.3 %copy.105 = bf16[1024,512]{1,0:T(8,128)(2,1)} copy(bf16[1024,512]{0,1:T(8,128)(2,1)S(1)} %bitcast.134) | data formatting | bytes 2097152
  (61 shorter events, 11.2 us)
Async XLA Ops:
  7.2 4.9 %copy-start = (bf16[1024,512]{1,0:T(8,128)(2,1)S(1)}, bf16[1024,512]{1,0:T(8,128)(2,1)}, u32[]{:S(2)}) copy-start(bf16[1024,512]{1,0:T(8,128)(2,1)} %param.8) | copy-start | bytes 3145732
  7.2 49.1 %all-gather.4.cloned.1.call-start = ((), (), s32[]{:S(2)}) async-start(), calls=%async_computation.3 | async-start | bytes 1179648 | tf_op jit(solution)/shard_map/all_gather | solution.py:48
  12.1 32.2 %copy-start.1 = (bf16[1024,512]{0,1:T(8,128)(2,1)}, bf16[1024,512]{0,1:T(8,128)(2,1)S(1)}, u32[]{:S(2)}) copy-start(bf16[1024,512]{0,1:T(8,128)(2,1)S(1)} %copy.83) | copy-start | bytes 3145732
  13.8 40.3 %all-to-all-start.1 = ((bf16[4,8,1]{0,2,1:T(2,128)(2,1)}), bf16[4,8,1]{0,2,1:T(2,128)(2,1)S(1)}, u32[]{:S(2)}, u32[]{:S(2)}) async-start(bf16[4,8,1]{0,2,1:T(2,128)(2,1)} %broadcast_in_dim.81), calls=%async_computation.1 | async-start | bytes 8192 | tf_op jit(solution)/shard_map/all_to_all | solution.py:100
  44.0 1.0 copy-start.5
  44.3 1.0 copy-start.8
  74.2 2.2 %copy-start.6 = (bf16[1024,512]{0,1:T(8,128)(2,1)S(1)}, bf16[1024,512]{0,1:T(8,128)(2,1)}, u32[]{:S(2)}) copy-start(bf16[1024,512]{0,1:T(8,128)(2,1)} %copy-done.5) | copy-start | bytes 3145732
  76.5 1.0 copy-start.3
  76.5 1.6 %copy-start.9 = (pred[1024,1024]{1,0:T(8,128)(4,1)S(1)}, pred[1024,1024]{1,0:T(8,128)(4,1)}, u32[]{:S(2)}) copy-start(pred[1024,1024]{1,0:T(8,128)(4,1)} %copy-done.8) | copy-start | bytes 3145732
  86.8 10.7 %all-to-all-start = ((bf16[4,8,2048]{2,0,1:T(4,128)(2,1)}), bf16[4,8,2048]{2,0,1:T(4,128)(2,1)S(1)}, u32[]{:S(2)}, u32[]{:S(2)}) async-start(bf16[4,8,2048]{2,0,1:T(4,128)(2,1)} %copy.96), calls=%async_computation | async-start | bytes 262144 | tf_op jit(solution)/shard_map/all_to_all | solution.py:93
  90.2 11.7 %copy-start.2 = (bf16[1024,512]{0,1:T(8,128)(2,1)S(1)}, bf16[1024,512]{0,1:T(8,128)(2,1)}, u32[]{:S(2)}) copy-start(bf16[1024,512]{0,1:T(8,128)(2,1)} %copy-done.1) | copy-start | bytes 3145732
  98.5 11.6 %all-to-all-start.2 = ((bf16[8,4,2048]{2,1,0:T(4,128)(2,1)}), bf16[8,4,2048]{2,1,0:T(4,128)(2,1)S(1)}, u32[]{:S(2)}, u32[]{:S(2)}) async-start(bf16[8,4,2048]{2,1,0:T(4,128)(2,1)} %copy.99), calls=%async_computation.2 | async-start | bytes 262144 | tf_op jit(solution)/shard_map/all_to_all | solution.py:107
  110.8 1.8 %copy-start.4 = (bf16[1024,4,128]{0,2,1:T(8,128)(2,1)S(1)}, bf16[1024,4,128]{0,2,1:T(8,128)(2,1)}, u32[]{:S(2)}) copy-start(bf16[1024,4,128]{0,2,1:T(8,128)(2,1)} %copy-done.3) | copy-start | bytes 3145732
  117.2 1.3 %copy-start.7 = (bf16[1024,512]{0,1:T(8,128)(2,1)S(1)}, bf16[1024,512]{0,1:T(8,128)(2,1)}, u32[]{:S(2)}) copy-start(bf16[1024,512]{0,1:T(8,128)(2,1)} %copy-done.5) | copy-start | bytes 3145732
Sparse Core Ops, SparseCore 0:
  13.3 42.9 all-gather.3
where the time goes:
time: 133 us; the launch traced here: 132 us
  matrix products  51.3 us (39%)
  blocking collectives  26.9 us (20%)
  between operations  14.3 us (11%)
  starting transfers between devices  14.1 us (11%)
  local copies, waits for them, and re-layouts  13.5 us (10%)
  waiting for transfers between devices  6.07 us (5%)
  other arithmetic  5.85 us (4%)
    all_gather x1, blocking collectives, body(): lax.all_gather(overall[None, :].astype(jnp.bfloat16), 'seq', axis=0, tile...  21 us
    unnamed x28, local copies, waits for them, and re-layouts  9.14 us
    dot_general x1, matrix products, body(): jnp.einsum('thv,shv->hts', output_delta, value_tile_block, preferred_elem...  7.87 us
    dot_general x1, matrix products, body(): jnp.einsum('hts,shv->thv', attn_weights, value_tile_block, preferred_elem...  7.76 us
    dot_general x1, matrix products, body(): jnp.einsum('thk,shk->hts', query_block, key_tile_block, preferred_element...  7.38 us
    all_to_all x1, starting transfers between devices, body(): lax.all_to_all(tiled.astype(jnp.bfloat16), 'seq', split_axis=1, concat_ax...  7.28 us
    dot_general x1, matrix products, body(): jnp.einsum('hts,shk->thk', mixed_half, key_tile_block, preferred_element_...  6.89 us
    psum x1, blocking collectives, body(): lax.psum((jnp.sum(output_result * output_result, axis=(1, 2)), jnp.sum(gr...  5.92 us
  transfers between devices with their start and end apart: 4, of which 2 were waited for; matrix products, arithmetic and copies ran while one was open for 18% of the time, Pallas kernels for 0%

commit v1 on v0

v1 whole, which is shorter than its diff:
```python
import functools

import jax
import jax.numpy as jnp
from jax import lax
from jax.experimental import pallas as pl
from jax.experimental.pallas import tpu as pltpu
from jax.sharding import PartitionSpec as P

EPS = 1e-06
F32 = jnp.float32
BF16 = jnp.bfloat16
MESH = pl.DeviceIdType.MESH


def dot(a, b, ca, cb, **kw):
    return lax.dot_general(
        a, b, (((ca,), (cb,)), ((), ())), preferred_element_type=F32, **kw
    )


def kernel(
    n, nh, H, T, D, C,
    rates, gate, q_hbm, k_hbm, v_hbm, g_hbm,
    dq_out, dk_out, dv_out,
    q, k, v, g, lrep, brow, bc, gown, gpeer,
    sl, w, o, macc, xacc, pstate, pchunk, sp,
    ubuf, upeer, cin, cout, stat, statin, tr,
    dob, vbuf, vpeer, din, dout, rl, dk1, dv1,
    in_sem, g_sem, us, ur, cs, cr, ss, sr, vs, vr, ds, dr,
):
    J = T // C
    LAST = n // 2 - 1
    me = lax.axis_index("seq")
    hd = lax.axis_index("head")
    inner = lax.rem(me, 2)
    z = me // 2
    peer = me + 1 - 2 * inner
    nxt = lax.rem(me + 2, n)
    prv = lax.rem(me + n - 2, n)

    def cols(h):
        start = h * D
        if not isinstance(h, int):
            start = pl.multiple_of(start, D)
        return pl.ds(start, D)

    def load(i, src, dst, h):
        return pltpu.make_async_copy(
            src.at[:, cols(h)], dst.at[:, cols(h)], in_sem.at[i, h]
        )

    for i, (src, dst) in enumerate(((k_hbm, k), (v_hbm, v), (q_hbm, q), (g_hbm, g))):
        for h in range(H):
            load(i, src, dst, h).start()

    barrier = pltpu.get_barrier_semaphore()
    for s in (peer, nxt, prv):
        pl.semaphore_signal(barrier, inc=1, device_id={"seq": s}, device_id_type=MESH)
    for d in range(1, nh):
        pl.semaphore_signal(
            barrier, inc=1, device_id={"head": lax.rem(hd + d, nh)}, device_id_type=MESH
        )

    def remote(src, dst, s_sem, r_sem, **to):
        return pltpu.make_async_remote_copy(
            src_ref=src, dst_ref=dst, send_sem=s_sem, recv_sem=r_sem,
            device_id=to, device_id_type=MESH,
        )

    l = -rates[...] * gate[...]
    for i in range(128 // H):
        lrep[i * H:(i + 1) * H, :] = l
    ri = lax.broadcasted_iota(jnp.int32, (C, C), 0)
    ci = lax.broadcasted_iota(jnp.int32, (C, C), 1)
    triu = jnp.where(ri <= ci, 1.0, 0.0).astype(F32)
    tot = [None] * H
    for j in range(J):
        r = dot(lrep[:, j * C:(j + 1) * C], triu, 1, 0, precision=lax.Precision.HIGHEST)
        brow[j] = r[0:8, :]
        col = r.T
        for h in range(H):
            b = jnp.broadcast_to(col[:, h:h + 1], (C, D))
            bc[h, j * C:(j + 1) * C, :] = b
            e = b[C - 1:C, :]
            tot[h] = e if tot[h] is None else tot[h] + e
    for h in range(H):
        gown[h:h + 1, :] = tot[h]

    gown[H:8, :] = jnp.zeros((8 - H, D), F32)
    pl.semaphore_wait(barrier, 3 + nh - 1)
    gcopy = remote(gown, gpeer, g_sem.at[0], g_sem.at[1], seq=peer)
    gcopy.start()

    def ucopy(h):
        return remote(ubuf.at[h], upeer.at[h], us.at[h], ur.at[h], seq=peer)

    def ccopy(h):
        return remote(cout.at[h], cin.at[h], cs.at[h], cr.at[h], seq=nxt)

    def vcopy(h):
        return remote(vbuf.at[h], vpeer.at[h], vs.at[h], vr.at[h], seq=peer)

    def dcopy(h):
        return remote(dout.at[h], din.at[h], ds.at[h], dr.at[h], seq=prv)

    def loop(lo, hi, fn):
        def step(h, carry):
            fn(h)
            return carry
        lax.fori_loop(lo, hi, step, 0)

    def rows(j):
        return slice(j * C, (j + 1) * C)

    def updates(h):
        load(0, k_hbm, k, h).wait()
        load(1, v_hbm, v, h).wait()
        s = jnp.zeros((D, D), F32)
        for j in range(J):
            b = bc[h, rows(j), :]
            e = b[C - 1:C, :]
            kd = (k[rows(j), cols(h)].astype(F32) * jnp.exp(e - b)).astype(BF16)
            u = dot(kd, v[rows(j), cols(h)], 0, 0)
            sl[h * (J + 1) + j] = s
            s = u if j == 0 else jnp.exp(e) * s + u
        sl[h * (J + 1) + J] = s
        ubuf[h] = s.astype(BF16)
        ucopy(h).start()

    loop(0, H, updates)

    def factor(h, j):
        b = bc[h, rows(j), :]
        left = jnp.concatenate([b] * (C // D), axis=1)
        right = brow[j, pl.ds(h, 1), :]
        return jnp.exp(jnp.where(ri >= ci, left - right, -jnp.inf))

    def intra(h):
        load(2, q_hbm, q, h).wait()
        for j in range(J):
            wj = dot(q[rows(j), cols(h)], k[rows(j), cols(h)], 1, 1) * factor(h, j)
            wj = wj.astype(BF16)
            w[h * J + j] = wj
            o[rows(j), cols(h)] = dot(wj, v[rows(j), cols(h)], 1, 0)

    half = H // 2
    loop(0, half, intra)
    gcopy.wait()

    def ex(ref, h):
        return jnp.exp(ref[pl.ds(h, 1), :])

    def pair(h):
        ucopy(h).wait_recv()
        own = sl[h * (J + 1) + J]

        @pl.when(inner == 0)
        def _():
            sp[h] = ex(gpeer, h) * own + upeer[h].astype(F32)

        @pl.when(inner == 1)
        def _():
            sp[h] = ex(gown, h) * upeer[h].astype(F32) + own

        @pl.when(z == 0)
        def _():
            cout[h] = sp[h].astype(BF16)
            cin[h] = jnp.zeros((D, D), BF16)

            @pl.when(z < LAST)
            def _():
                ccopy(h).start()

    loop(0, H, pair)
    loop(half, H, intra)
    for h in range(H):
        load(3, g_hbm, g, h).wait()

    def chain(h):
        @pl.when(z > 0)
        def _():
            ccopy(h).wait_recv()

            @pl.when(z < LAST)
            def _():
                a = ex(gown, h) * ex(gpeer, h)
                cout[h] = (a * cin[h].astype(F32) + sp[h]).astype(BF16)
                ccopy(h).start()

        @pl.when(inner == 0)
        def _():
            pstate[h] = cin[h].astype(F32)

        @pl.when(inner == 1)
        def _():
            pstate[h] = ex(gpeer, h) * cin[h].astype(F32) + upeer[h].astype(F32)

        s = pstate[h]
        for j in range(J):
            pj = (s + sl[h * (J + 1) + j] if j else s).astype(BF16)
            pchunk[h * J + j] = pj
            b = bc[h, rows(j), :]
            s = s * jnp.exp(b[C - 1:C, :])
            qe = (q[rows(j), cols(h)].astype(F32) * jnp.exp(b)).astype(BF16)
            oj = o[rows(j), cols(h)] + dot(qe, pj, 1, 0)
            o[rows(j), cols(h)] = oj
            gj = g[rows(j), cols(h)].astype(F32)

            @pl.when(h == 0)
            def _():
                macc[rows(j), :] = oj * oj
                xacc[rows(j), :] = gj * oj

            @pl.when(h > 0)
            def _():
                macc[rows(j), :] += oj * oj
                xacc[rows(j), :] += gj * oj

    loop(0, H, chain)

    NG = T // 128
    lane = lax.broadcasted_iota(jnp.int32, (128, 128), 1)
    acc = jnp.zeros((128, 128), F32)
    for u in range(NG):
        part = slice(u * 128, (u + 1) * 128)
        acc = jnp.where(lane == u, jnp.sum(macc[part, :], axis=1, keepdims=True), acc)
        acc = jnp.where(lane == NG + u, jnp.sum(xacc[part, :], axis=1, keepdims=True), acc)
    stat[...] = acc.T[0:2 * NG, :]
    scopies = [
        remote(stat, statin.at[d - 1], ss.at[d - 1], sr.at[d - 1], head=lax.rem(hd + d, nh))
        for d in range(1, nh)
    ]
    for c in scopies:
        c.start()
    for c in scopies:
        c.wait_recv()
    whole = stat[...]
    for d in range(nh - 1):
        whole = whole + statin[d]
    width = float(H * nh * D)
    root = jnp.sqrt(whole[0:NG] / width + EPS)
    tr[...] = jnp.zeros_like(tr)
    tr[0:NG, :] = 1.0 / root
    tr[NG:2 * NG, :] = whole[NG:2 * NG] / (width * root * root * root)
    back = tr[...].T
    for u in range(NG):
        part = slice(u * 128, (u + 1) * 128)
        macc[part, :] = jnp.broadcast_to(back[:, u:u + 1], (128, D))
        xacc[part, :] = jnp.broadcast_to(back[:, NG + u:NG + u + 1], (128, D))

    def outgrad(h):
        s = None
        for j in reversed(range(J)):
            do = (
                g[rows(j), cols(h)].astype(F32) * macc[rows(j), :]
                - o[rows(j), cols(h)] * xacc[rows(j), :]
            ).astype(BF16)
            dob[rows(j), cols(h)] = do
            b = bc[h, rows(j), :]
            qe = (q[rows(j), cols(h)].astype(F32) * jnp.exp(b)).astype(BF16)
            u = dot(qe, do, 0, 0)
            rl[h * (J + 1) + j + 1] = jnp.zeros((D, D), F32) if s is None else s
            s = u if s is None else u + jnp.exp(b[C - 1:C, :]) * s
        rl[h * (J + 1)] = s
        vbuf[h] = s.astype(BF16)
        vcopy(h).start()

    loop(0, H, outgrad)

    def grads(h):
        for j in range(J):
            do = dob[rows(j), cols(h)]
            e = (dot(do, v[rows(j), cols(h)], 1, 1) * factor(h, j)).astype(BF16)
            eb = jnp.exp(bc[h, rows(j), :])
            dq_out[rows(j), cols(h)] = (
                eb * dot(do, pchunk[h * J + j], 1, 1) + dot(e, k[rows(j), cols(h)], 1, 0)
            ).astype(BF16)
            dk1[rows(j), cols(h)] = dot(e, q[rows(j), cols(h)], 0, 0)
            dv1[rows(j), cols(h)] = dot(w[h * J + j], do, 0, 0)

    loop(0, half, grads)

    def pair_back(h):
        vcopy(h).wait_recv()
        own = rl[h * (J + 1)]

        @pl.when(inner == 0)
        def _():
            sp[h] = own + ex(gown, h) * vpeer[h].astype(F32)

        @pl.when(inner == 1)
        def _():
            sp[h] = vpeer[h].astype(F32) + ex(gpeer, h) * own

        @pl.when(z == LAST)
        def _():
            dout[h] = sp[h].astype(BF16)
            din[h] = jnp.zeros((D, D), BF16)

            @pl.when(z > 0)
            def _():
                dcopy(h).start()

    loop(0, H, pair_back)
    loop(half, H, grads)

    def chain_back(h):
        @pl.when(z < LAST)
        def _():
            dcopy(h).wait_recv()

            @pl.when(z > 0)
            def _():
                a = ex(gown, h) * ex(gpeer, h)
                dout[h] = (a * din[h].astype(F32) + sp[h]).astype(BF16)
                dcopy(h).start()

        @pl.when(inner == 1)
        def _():
            pstate[h] = din[h].astype(F32)

        @pl.when(inner == 0)
        def _():
            pstate[h] = ex(gpeer, h) * din[h].astype(F32) + vpeer[h].astype(F32)

        s = pstate[h]
        for j in reversed(range(J)):
            rj = (s + rl[h * (J + 1) + j + 1] if j < J - 1 else s).astype(BF16)
            b = bc[h, rows(j), :]
            e = b[C - 1:C, :]
            s = s * jnp.exp(e)
            tail = jnp.exp(e - b)
            dk_out[rows(j), cols(h)] = (
                dk1[rows(j), cols(h)] + tail * dot(v[rows(j), cols(h)], rj, 1, 1)
            ).astype(BF16)
            dv_out[rows(j), cols(h)] = (
                dv1[rows(j), cols(h)] + tail * dot(k[rows(j), cols(h)], rj, 1, 0)
            ).astype(BF16)

    loop(0, H, chain_back)

    for c in scopies:
        c.wait_send()

    def drain(h):
        ucopy(h).wait_send()
        vcopy(h).wait_send()

        @pl.when(z < LAST)
        def _():
            ccopy(h).wait_send()

        @pl.when(z > 0)
        def _():
            dcopy(h).wait_send()

    loop(0, H, drain)


def body(queries, key_vectors, value_vectors, out_grad, head_rates, gate_scale):
    H, T = gate_scale.shape
    D = queries.shape[1] // H
    n = lax.axis_size("seq")
    nh = lax.axis_size("head")
    C = min(256, T)
    J = T // C
    tile = pltpu.VMEM((H, D, D), BF16)
    full = pltpu.VMEM((T, H * D), BF16)
    wide = pltpu.VMEM((T, H * D), F32)
    sem = pltpu.SemaphoreType.DMA
    out = jax.ShapeDtypeStruct((T, H * D), BF16)
    vm = pl.BlockSpec(memory_space=pltpu.VMEM)
    hbm = pl.BlockSpec(memory_space=pl.ANY)
    return pl.pallas_call(
        functools.partial(kernel, n, nh, H, T, D, C),
        out_shape=(out, out, out),
        in_specs=[vm, vm, hbm, hbm, hbm, hbm],
        out_specs=(vm, vm, vm),
        scratch_shapes=[
            full, full, full, full,
            pltpu.VMEM((128, T), F32),
            pltpu.VMEM((J, 8, C), F32),
            pltpu.VMEM((H, T, D), F32),
            pltpu.VMEM((8, D), F32),
            pltpu.VMEM((8, D), F32),
            pltpu.VMEM((H * (J + 1), D, D), F32),
            pltpu.VMEM((H * J, C, C), BF16),
            wide,
            pltpu.VMEM((T, D), F32),
            pltpu.VMEM((T, D), F32),
            pltpu.VMEM((H, D, D), F32),
            pltpu.VMEM((H * J, D, D), BF16),
            pltpu.VMEM((H, D, D), F32),
            tile, tile, tile, tile,
            pltpu.VMEM((2 * T // 128, 128), F32),
            pltpu.VMEM((nh - 1, 2 * T // 128, 128), F32),
            pltpu.VMEM((128, 128), F32),
            full,
            tile, tile, tile, tile,
            pltpu.VMEM((H * (J + 1), D, D), F32),
            wide, wide,
            sem((4, H)), sem((2,)),
            sem((H,)), sem((H,)), sem((H,)), sem((H,)),
            sem((nh - 1,)), sem((nh - 1,)),
            sem((H,)), sem((H,)), sem((H,)), sem((H,)),
        ],
        compiler_params=pltpu.CompilerParams(
            collective_id=0, has_side_effects=True, vmem_limit_bytes=44 * 1024 * 1024
        ),
    )(head_rates[:, None], gate_scale, queries, key_vectors, value_vectors, out_grad)


def solution(mesh):
    placed = (
        P("seq", "head"),
        P("seq", "head"),
        P("seq", "head"),
        P("seq", "head"),
        P("head"),
        P("head", "seq"),
    )
    return jax.shard_map(
        body,
        mesh=mesh,
        in_specs=placed,
        out_specs=(P("seq", "head"), P("seq", "head"), P("seq", "head")),
        check_vma=False,
    )
```

time: 133 us -> 51.8 us (0.39)
  matrix products: 51.3 us -> 0 us
  Pallas kernels: 0 us -> 41.6 us
  blocking collectives: 26.9 us -> 0 us
  starting transfers between devices: 14.1 us -> 0 us
  between operations: 14.3 us -> 0.65 us
  waiting for transfers between devices: 6.07 us -> 0 us
  other arithmetic: 5.85 us -> 0 us
  local copies, waits for them, and re-layouts: 13.5 us -> 9.27 us
    dot_general x14 -> x0, matrix products: 51.3 us -> none  [the longest x1 7.87 us: body(): jnp.einsum('thv,shv->hts', output_delta, value_tile_block, preferred_elem...]
    pallas_call x0 -> x1, Pallas kernels: none -> 41.6 us  [body(): pl.pallas_call(functools.partial(kernel, n, nh, H, T, D, C), out_shape=(o...]
    all_gather x1 -> x0, blocking collectives: 21 us -> none  [body(): lax.all_gather(overall[None, :].astype(jnp.bfloat16), 'seq', axis=0, tile...]
    all_to_all x3 -> x0, starting transfers between devices: 14 us -> none  [the longest x1 7.28 us: body(): lax.all_to_all(tiled.astype(jnp.bfloat16), 'seq', split_axis=1, concat_ax...]
    psum x1 -> x0, blocking collectives: 5.92 us -> none  [body(): lax.psum((jnp.sum(output_result * output_result, axis=(1, 2)), jnp.sum(gr...]
    all_to_all x3 -> x0, waiting for transfers between devices: 4.19 us -> none  [the longest x1 4.19 us: body(): lax.all_to_all(gradient_total_sum.reshape(heads, -1).astype(jnp.bfloat16)...]
    convert_element_type x6 -> x0, local copies, waits for them, and re-layouts: 3.22 us -> none  [the longest x1 1.48 us: body(): grad_full = grad_block.astype(jnp.float32)]
    convert_element_type x4 -> x0, other arithmetic: 2.22 us -> none  [the longest x1 2.21 us: body(): output_delta = output_delta.astype(jnp.bfloat16)]
  transfers between devices with their start and end apart: 4 -> 0, of which waited for: 2 -> 0; matrix products, arithmetic and copies ran while one was open for 18% -> 0% of each run, Pallas kernels for 0% -> 0%
where the time goes in v1:
time: 51.8 us; the launch traced here: 51.5 us
  Pallas kernels  41.6 us (80%)
  local copies, waits for them, and re-layouts  9.27 us (18%)
  between operations  0.65 us (1%)
    pallas_call x1, Pallas kernels, body(): pl.pallas_call(functools.partial(kernel, n, nh, H, T, D, C), out_shape=(o...  41.6 us
    unnamed x15, local copies, waits for them, and re-layouts  9.17 us

profile of v1, /device:TPU:0, one launch (start us, length us, event | category | flops | bytes accessed | tf_op | source)
XLA Modules:
  0.0 51.5 jit_solution(3393264775032051326)
XLA Ops:
  0.6 0.0 copy-start.5
  0.6 0.6 %copy-done.5 = f32[4]{0:T(128)S(1)} copy-done((f32[4]{0:T(128)S(1)}, f32[4]{0:T(128)}, u32[]{:S(2)}) %copy-start.5) | copy-done | bytes 40
  1.3 0.1 copy.9.rates
  1.4 0.0 copy-start
  1.4 1.2 %copy-done = bf16[1024,512]{1,0:T(8,128)(2,1)S(1)} copy-done((bf16[1024,512]{1,0:T(8,128)(2,1)S(1)}, bf16[1024,512]{1,0:T(8,128)(2,1)}, u32[]{:S(2)}) %copy-start) | copy-done | bytes 1048600
  2.6 0.0 copy-start.1
  2.6 1.2 %copy-done.1 = bf16[1024,512]{1,0:T(8,128)(2,1)S(1)} copy-done((bf16[1024,512]{1,0:T(8,128)(2,1)S(1)}, bf16[1024,512]{1,0:T(8,128)(2,1)}, u32[]{:S(2)}) %copy-start.1) | copy-done | bytes 1048600
  3.8 0.0 copy-start.2
  3.8 1.2 %copy-done.2 = bf16[1024,512]{1,0:T(8,128)(2,1)S(1)} copy-done((bf16[1024,512]{1,0:T(8,128)(2,1)S(1)}, bf16[1024,512]{1,0:T(8,128)(2,1)}, u32[]{:S(2)}) %copy-start.2) | copy-done | bytes 1048600
  5.1 0.0 copy-start.3
  5.1 1.2 %copy-done.3 = bf16[1024,512]{1,0:T(8,128)(2,1)S(1)} copy-done((bf16[1024,512]{1,0:T(8,128)(2,1)S(1)}, bf16[1024,512]{1,0:T(8,128)(2,1)}, u32[]{:S(2)}) %copy-start.3) | copy-done | bytes 1048600
  6.3 0.0 copy-start.4
  6.3 0.7 %copy-done.4 = f32[4,1024]{1,0:T(4,128)S(1)} copy-done((f32[4,1024]{1,0:T(4,128)S(1)}, f32[4,1024]{1,0:T(4,128)}, u32[]{:S(2)}) %copy-start.4) | copy-done | bytes 16408
  7.0 41.6 %shard_map.85 = (bf16[1024,512]{1,0:T(8,128)(2,1)S(1)}, bf16[1024,512]{1,0:T(8,128)(2,1)S(1)}, bf16[1024,512]{1,0:T(8,128)(2,1)S(1)}) custom-call(f32[4,1]{1,0:T(4,128)S(1)} %copy.9.rates, f32[4,1024]{1,0:T(4,128)S(1)} %copy-done.4, bf16[1024,512]{1,0:T(8,128)(2,1)S(1)} %copy-done, bf16[1024,512]{1,0:T(8,128)(2,1)S(1)} %copy-done.1, ...), custom_call_target="tpu_custom_call" | custom-call | tf_op jit(solution)/shard_map/pallas_call | solution.py:375
  48.6 1.0 %copy.13 = bf16[1024,512]{1,0:T(8,128)(2,1)} copy(bf16[1024,512]{1,0:T(8,128)(2,1)S(1)} %get-tuple-element.6) | data formatting | bytes 2097152
  49.6 1.0 %copy.14 = bf16[1024,512]{1,0:T(8,128)(2,1)} copy(bf16[1024,512]{1,0:T(8,128)(2,1)S(1)} %get-tuple-element.7) | data formatting | bytes 2097152
  50.5 1.0 %copy.15 = bf16[1024,512]{1,0:T(8,128)(2,1)} copy(bf16[1024,512]{1,0:T(8,128)(2,1)S(1)} %get-tuple-element.8) | data formatting | bytes 2097152
Async XLA Ops:
  0.6 0.7 %copy-start.5 = (f32[4]{0:T(128)S(1)}, f32[4]{0:T(128)}, u32[]{:S(2)}) copy-start(f32[4]{0:T(128)} %param.10) | copy-start | bytes 52
  1.4 1.2 %copy-start = (bf16[1024,512]{1,0:T(8,128)(2,1)S(1)}, bf16[1024,512]{1,0:T(8,128)(2,1)}, u32[]{:S(2)}) copy-start(bf16[1024,512]{1,0:T(8,128)(2,1)} %q_hbm.1) | copy-start | bytes 3145732
  2.6 1.2 %copy-start.1 = (bf16[1024,512]{1,0:T(8,128)(2,1)S(1)}, bf16[1024,512]{1,0:T(8,128)(2,1)}, u32[]{:S(2)}) copy-start(bf16[1024,512]{1,0:T(8,128)(2,1)} %k_hbm.1) | copy-start | bytes 3145732
  3.8 1.2 %copy-start.2 = (bf16[1024,512]{1,0:T(8,128)(2,1)S(1)}, bf16[1024,512]{1,0:T(8,128)(2,1)}, u32[]{:S(2)}) copy-start(bf16[1024,512]{1,0:T(8,128)(2,1)} %v_hbm.1) | copy-start | bytes 3145732
  5.1 1.2 %copy-start.3 = (bf16[1024,512]{1,0:T(8,128)(2,1)S(1)}, bf16[1024,512]{1,0:T(8,128)(2,1)}, u32[]{:S(2)}) copy-start(bf16[1024,512]{1,0:T(8,128)(2,1)} %g_hbm.1) | copy-start | bytes 3145732
  6.3 0.7 %copy-start.4 = (f32[4,1024]{1,0:T(4,128)S(1)}, f32[4,1024]{1,0:T(4,128)}, u32[]{:S(2)}) copy-start(f32[4,1024]{1,0:T(4,128)} %gate.1) | copy-start | bytes 49156

commit v2 on v1

--- a/solution.py
+++ b/solution.py
@@ -21,13 +21,13 @@
 
 def kernel(
     n, nh, H, T, D, C,
-    rates, gate, q_hbm, k_hbm, v_hbm, g_hbm,
+    rates, gate_hbm, q_hbm, k_hbm, v_hbm, g_hbm,
     dq_out, dk_out, dv_out,
-    q, k, v, g, lrep, brow, bc, gown, gpeer,
+    gate, q, k, v, g, lrep, brow, bc, gown, gpeer,
     sl, w, o, macc, xacc, pstate, pchunk, sp,
     ubuf, upeer, cin, cout, stat, statin, tr,
     dob, vbuf, vpeer, din, dout, rl, dk1, dv1,
-    in_sem, g_sem, us, ur, cs, cr, ss, sr, vs, vr, ds, dr,
+    in_sem, gate_sem, g_sem, us, ur, cs, cr, ss, sr, vs, vr, ds, dr,
 ):
     J = T // C
     LAST = n // 2 - 1
@@ -50,6 +50,8 @@
             src.at[:, cols(h)], dst.at[:, cols(h)], in_sem.at[i, h]
         )
 
+    gate_copy = pltpu.make_async_copy(gate_hbm, gate, gate_sem.at[0])
+    gate_copy.start()
     for i, (src, dst) in enumerate(((k_hbm, k), (v_hbm, v), (q_hbm, q), (g_hbm, g))):
         for h in range(H):
             load(i, src, dst, h).start()
@@ -68,15 +70,21 @@
             device_id=to, device_id_type=MESH,
         )
 
-    l = -rates[...] * gate[...]
+    gate_copy.wait()
+    l = jnp.concatenate([gate[h:h + 1, :] * -rates[h] for h in range(H)], axis=0)
     for i in range(128 // H):
         lrep[i * H:(i + 1) * H, :] = l
     ri = lax.broadcasted_iota(jnp.int32, (C, C), 0)
     ci = lax.broadcasted_iota(jnp.int32, (C, C), 1)
-    triu = jnp.where(ri <= ci, 1.0, 0.0).astype(F32)
+    triu = jnp.where(ri <= ci, 1.0, 0.0).astype(BF16)
     tot = [None] * H
     for j in range(J):
-        r = dot(lrep[:, j * C:(j + 1) * C], triu, 1, 0, precision=lax.Precision.HIGHEST)
+        lj = lrep[:, j * C:(j + 1) * C]
+        hi = lj.astype(BF16)
+        rest = lj - hi.astype(F32)
+        mid = rest.astype(BF16)
+        low = (rest - mid.astype(F32)).astype(BF16)
+        r = dot(low, triu, 1, 0) + dot(mid, triu, 1, 0) + dot(hi, triu, 1, 0)
         brow[j] = r[0:8, :]
         col = r.T
         for h in range(H):
@@ -369,15 +377,16 @@
     full = pltpu.VMEM((T, H * D), BF16)
     wide = pltpu.VMEM((T, H * D), F32)
     sem = pltpu.SemaphoreType.DMA
-    out = jax.ShapeDtypeStruct((T, H * D), BF16)
+    out = pltpu.VMEM((T, H * D), BF16)
     vm = pl.BlockSpec(memory_space=pltpu.VMEM)
     hbm = pl.BlockSpec(memory_space=pl.ANY)
     return pl.pallas_call(
         functools.partial(kernel, n, nh, H, T, D, C),
         out_shape=(out, out, out),
-        in_specs=[vm, vm, hbm, hbm, hbm, hbm],
+        in_specs=[pl.BlockSpec(memory_space=pltpu.SMEM), hbm, hbm, hbm, hbm, hbm],
         out_specs=(vm, vm, vm),
         scratch_shapes=[
+            pltpu.VMEM((H, T), F32),
             full, full, full, full,
             pltpu.VMEM((128, T), F32),
             pltpu.VMEM((J, 8, C), F32),
@@ -400,15 +409,15 @@
             tile, tile, tile, tile,
             pltpu.VMEM((H * (J + 1), D, D), F32),
             wide, wide,
-            sem((4, H)), sem((2,)),
+            sem((4, H)), sem((1,)), sem((2,)),
             sem((H,)), sem((H,)), sem((H,)), sem((H,)),
             sem((nh - 1,)), sem((nh - 1,)),
             sem((H,)), sem((H,)), sem((H,)), sem((H,)),
         ],
         compiler_params=pltpu.CompilerParams(
-            collective_id=0, has_side_effects=True, vmem_limit_bytes=44 * 1024 * 1024
+            collective_id=0, has_side_effects=True, vmem_limit_bytes=63692800
         ),
-    )(head_rates[:, None], gate_scale, queries, key_vectors, value_vectors, out_grad)
+    )(head_rates, gate_scale, queries, key_vectors, value_vectors, out_grad)
 
 
 def solution(mesh):

time: 51.8 us -> 45.6 us (0.88)
  local copies, waits for them, and re-layouts: 9.27 us -> 2.91 us
    unnamed x15 -> x3, local copies, waits for them, and re-layouts: 9.17 us -> 2.91 us
where the time goes in v2:
time: 45.6 us; the launch traced here: 45.4 us
  Pallas kernels  41.8 us (92%)
  local copies, waits for them, and re-layouts  2.91 us (6%)
  between operations  0.64 us (1%)
    pallas_call x1, Pallas kernels, body(): pl.pallas_call(functools.partial(kernel, n, nh, H, T, D, C), out_shape=(o...  41.8 us
    unnamed x3, local copies, waits for them, and re-layouts  2.91 us

profile of v2, /device:TPU:0, one launch (start us, length us, event | category | flops | bytes accessed | tf_op | source)
XLA Modules:
  0.0 45.4 jit_solution(5557733612016899395)
XLA Ops:
  0.6 41.8 %shard_map.85 = (bf16[1024,512]{1,0:T(8,128)(2,1)S(1)}, bf16[1024,512]{1,0:T(8,128)(2,1)S(1)}, bf16[1024,512]{1,0:T(8,128)(2,1)S(1)}) custom-call(f32[4]{0:T(128)} %rates.1, f32[4,1024]{1,0:T(4,128)} %gate_hbm.1, bf16[1024,512]{1,0:T(8,128)(2,1)} %q_hbm.1, bf16[1024,512]{1,0:T(8,128)(2,1)} %k_hbm.1, bf16[1024,512]{1,0:T(8,128)(2,1)} %v_hbm.1, ...), custom_call_target="tpu_custom_call" | custom-call | tf_op jit(solution)/shard_map/pallas_call | solution.py:383
  42.5 1.0 %copy.12 = bf16[1024,512]{1,0:T(8,128)(2,1)} copy(bf16[1024,512]{1,0:T(8,128)(2,1)S(1)} %get-tuple-element.3) | data formatting | bytes 2097152
  43.5 1.0 %copy.13 = bf16[1024,512]{1,0:T(8,128)(2,1)} copy(bf16[1024,512]{1,0:T(8,128)(2,1)S(1)} %get-tuple-element.4) | data formatting | bytes 2097152
  44.4 1.0 %copy.14 = bf16[1024,512]{1,0:T(8,128)(2,1)} copy(bf16[1024,512]{1,0:T(8,128)(2,1)S(1)} %get-tuple-element.5) | data formatting | bytes 2097152

commit v3 on v2

--- a/solution.py
+++ b/solution.py
@@ -103,14 +103,19 @@
     def ucopy(h):
         return remote(ubuf.at[h], upeer.at[h], us.at[h], ur.at[h], seq=peer)
 
-    def ccopy(h):
-        return remote(cout.at[h], cin.at[h], cs.at[h], cr.at[h], seq=nxt)
+    half_rows = D // 2
+    pieces = tuple(slice(p * half_rows, (p + 1) * half_rows) for p in range(2))
+
+    def ccopy(h, p):
+        part = pl.ds(p * half_rows, half_rows)
+        return remote(cout.at[h, part], cin.at[h, part], cs.at[h, p], cr.at[h, p], seq=nxt)
 
     def vcopy(h):
         return remote(vbuf.at[h], vpeer.at[h], vs.at[h], vr.at[h], seq=peer)
 
-    def dcopy(h):
-        return remote(dout.at[h], din.at[h], ds.at[h], dr.at[h], seq=prv)
+    def dcopy(h, p):
+        part = pl.ds(p * half_rows, half_rows)
+        return remote(dout.at[h, part], din.at[h, part], ds.at[h, p], dr.at[h, p], seq=prv)
 
     def loop(lo, hi, fn):
         def step(h, carry):
@@ -178,7 +183,8 @@
 
             @pl.when(z < LAST)
             def _():
-                ccopy(h).start()
+                for p in range(2):
+                    ccopy(h, p).start()
 
     loop(0, H, pair)
     loop(half, H, intra)
@@ -188,13 +194,16 @@
     def chain(h):
         @pl.when(z > 0)
         def _():
-            ccopy(h).wait_recv()
-
-            @pl.when(z < LAST)
-            def _():
-                a = ex(gown, h) * ex(gpeer, h)
-                cout[h] = (a * cin[h].astype(F32) + sp[h]).astype(BF16)
-                ccopy(h).start()
+            for p, part in enumerate(pieces):
+                ccopy(h, p).wait_recv()
+
+                @pl.when(z < LAST)
+                def _():
+                    a = ex(gown, h) * ex(gpeer, h)
+                    cout[h, part, :] = (
+                        a * cin[h, part, :].astype(F32) + sp[h, part, :]
+                    ).astype(BF16)
+                    ccopy(h, p).start()
 
         @pl.when(inner == 0)
         def _():
@@ -308,7 +317,8 @@
 
             @pl.when(z > 0)
             def _():
-                dcopy(h).start()
+                for p in range(2):
+                    dcopy(h, p).start()
 
     loop(0, H, pair_back)
     loop(half, H, grads)
@@ -316,13 +326,16 @@
     def chain_back(h):
         @pl.when(z < LAST)
         def _():
-            dcopy(h).wait_recv()
-
-            @pl.when(z > 0)
-            def _():
-                a = ex(gown, h) * ex(gpeer, h)
-                dout[h] = (a * din[h].astype(F32) + sp[h]).astype(BF16)
-                dcopy(h).start()
+            for p, part in enumerate(pieces):
+                dcopy(h, p).wait_recv()
+
+                @pl.when(z > 0)
+                def _():
+                    a = ex(gown, h) * ex(gpeer, h)
+                    dout[h, part, :] = (
+                        a * din[h, part, :].astype(F32) + sp[h, part, :]
+                    ).astype(BF16)
+                    dcopy(h, p).start()
 
         @pl.when(inner == 1)
         def _():
@@ -357,11 +370,13 @@
 
         @pl.when(z < LAST)
         def _():
-            ccopy(h).wait_send()
+            for p in range(2):
+                ccopy(h, p).wait_send()
 
         @pl.when(z > 0)
         def _():
-            dcopy(h).wait_send()
+            for p in range(2):
+                dcopy(h, p).wait_send()
 
     loop(0, H, drain)
 
@@ -410,9 +425,9 @@
             pltpu.VMEM((H * (J + 1), D, D), F32),
             wide, wide,
             sem((4, H)), sem((1,)), sem((2,)),
-            sem((H,)), sem((H,)), sem((H,)), sem((H,)),
+            sem((H,)), sem((H,)), sem((H, 2)), sem((H, 2)),
             sem((nh - 1,)), sem((nh - 1,)),
-            sem((H,)), sem((H,)), sem((H,)), sem((H,)),
+            sem((H,)), sem((H,)), sem((H, 2)), sem((H, 2)),
         ],
         compiler_params=pltpu.CompilerParams(
             collective_id=0, has_side_effects=True, vmem_limit_bytes=63692800

time: 45.6 us -> 45.4 us (level)
  no operation moved by 1% of the time
where the time goes in v3:
time: 45.4 us; the launch traced here: 45.2 us
  Pallas kernels  41.7 us (92%)
  local copies, waits for them, and re-layouts  2.91 us (6%)
  between operations  0.64 us (1%)
    pallas_call x1, Pallas kernels, body(): pl.pallas_call(functools.partial(kernel, n, nh, H, T, D, C), out_shape=(o...  41.7 us
    unnamed x3, local copies, waits for them, and re-layouts  2.91 us

profile of v3, /device:TPU:0, one launch (start us, length us, event | category | flops | bytes accessed | tf_op | source)
XLA Modules:
  0.0 45.2 jit_solution(464201154684799336)
XLA Ops:
  0.6 41.7 %shard_map.85 = (bf16[1024,512]{1,0:T(8,128)(2,1)S(1)}, bf16[1024,512]{1,0:T(8,128)(2,1)S(1)}, bf16[1024,512]{1,0:T(8,128)(2,1)S(1)}) custom-call(f32[4]{0:T(128)} %rates.1, f32[4,1024]{1,0:T(4,128)} %gate_hbm.1, bf16[1024,512]{1,0:T(8,128)(2,1)} %q_hbm.1, bf16[1024,512]{1,0:T(8,128)(2,1)} %k_hbm.1, bf16[1024,512]{1,0:T(8,128)(2,1)} %v_hbm.1, ...), custom_call_target="tpu_custom_call" | custom-call | tf_op jit(solution)/shard_map/pallas_call | solution.py:398
  42.3 1.0 %copy.12 = bf16[1024,512]{1,0:T(8,128)(2,1)} copy(bf16[1024,512]{1,0:T(8,128)(2,1)S(1)} %get-tuple-element.3) | data formatting | bytes 2097152
  43.3 1.0 %copy.13 = bf16[1024,512]{1,0:T(8,128)(2,1)} copy(bf16[1024,512]{1,0:T(8,128)(2,1)S(1)} %get-tuple-element.4) | data formatting | bytes 2097152
  44.3 1.0 %copy.14 = bf16[1024,512]{1,0:T(8,128)(2,1)} copy(bf16[1024,512]{1,0:T(8,128)(2,1)S(1)} %get-tuple-element.5) | data formatting | bytes 2097152
